TPU v7x, 32 devices: a 4x4x1 block of a 4x4x8 slice. The times are simulated.
32 devices in a mesh: batch: 1 (over z), row: 4 (over y), col: 8 (over x, core).
Axes of the slice: x: 4, y: 4, z: 1, core: 2. Of those that a mesh axis runs over, the one named last changes fastest.
The devices are a block of a 4x4x8 slice.
Arguments:
- l_mat: bfloat16 [2048, 2048], P(('batch', 'row'), 'col')
- b_mat: bfloat16 [2048, 65536], P(('batch', 'row'), 'col')
Outputs:
- output: bfloat16 [2048, 65536], P(('batch', 'row'), 'col')
All inputs are finite; a program needn't handle non-finite values.
Results may differ from a plain program's by a relative error of at most 0.001.
Values are sent between devices in bfloat16 or wider.
A program may use at most 768 MiB of HBM per device.

v0:
```python
import jax
import jax.numpy as jnp
from jax import lax
from jax.sharding import PartitionSpec as P


def solution(mesh):
    block_spec = P(('batch', 'row'), 'col')

    def local_product(l_block, b_block):
        l_strip = lax.all_gather(l_block, 'col', axis=1, tiled=True)
        b_strip = lax.all_gather(b_block, 'row', axis=0, tiled=True)
        result = jnp.dot(l_strip, b_strip, preferred_element_type=jnp.float32)
        return result.astype(b_block.dtype)

    return jax.shard_map(local_product, mesh=mesh, in_specs=(block_spec, block_spec), out_specs=block_spec, check_vma=False)
```

profile of v0, /device:TPU:112, one launch (start us, length us, event | category | flops | bytes accessed | tf_op | source)
XLA Modules:
  0.0 361.5 jit_solution(12268205723558669454)
XLA Ops:
  6.5 0.0 all-gather.3.cloned.1.call-start
  6.6 0.7 all-gather.3.cloned.1.call-update
  7.3 0.1 all-gather.5.cloned.1.call-start
  7.4 0.7 all-gather.5.cloned.1.call-update
  8.1 26.6 %all-gather.3.cloned.1.call-done = bf16[512,2048]{1,0:T(8,128)(2,1)} async-done(((bf16[512,256]{1,0:T(8,128)(2,1)}), bf16[512,2048]{1,0:T(8,128)(2,1)}) %all-gather.3.cloned.1.call-update) | async-done | bytes 2097168 | tf_op jit(solution)/shard_map/all_gather | solution.py:11
  34.7 293.9 %all-gather.5.cloned.1.call-done = bf16[2048,8192]{1,0:T(8,128)(2,1)} async-done(((bf16[512,8192]{1,0:T(8,128)(2,1)}), bf16[2048,8192]{1,0:T(8,128)(2,1)}) %all-gather.5.cloned.1.call-update) | async-done | bytes 33554448 | tf_op jit(solution)/shard_map/all_gather | solution.py:12
  328.7 26.0 %convolution_convert_fusion = bf16[512,8192]{1,0:T(8,128)(2,1)} fusion(bf16[512,2048]{1,0:T(8,128)(2,1)} %all-gather.3.cloned.1.call-done, bf16[2048,8192]{1,0:T(8,128)(2,1)} %all-gather.5.cloned.1.call-done), kind=kOutput, calls=%fused_computation | convolution fusion | flops 17184063488 | bytes 44040192 | tf_op jit(solution)/shard_map/dot_general | solution.py:13
Async XLA Ops:
  6.5 28.2 %all-gather.3.cloned.1.call-start = ((), (), s32[]{:S(2)}) async-start(), calls=%async_computation | async-start | bytes 2359296 | tf_op jit(solution)/shard_map/all_gather | solution.py:11
  7.3 321.3 %all-gather.5.cloned.1.call-start = ((), (), s32[]{:S(2)}) async-start(), calls=%async_computation.1 | async-start | bytes 41943040 | tf_op jit(solution)/shard_map/all_gather | solution.py:12
Sparse Core Ops, SparseCore 0:
  8.9 25.7 all-gather.2
  36.3 292.3 all-gather.4
where the time goes:
time: 364 us; the launch traced here: 362 us
  waiting for transfers between devices  322 us (88%)
  matrix products  26 us (7%)
  between operations  13.4 us (4%)
    all_gather x1, waiting for transfers between devices, local_product(): b_strip = lax.all_gather(b_block, 'row', axis=0, tiled=True)  294 us
    all_gather x1, waiting for transfers between devices, local_product(): l_strip = lax.all_gather(l_block, 'col', axis=1, tiled=True)  26.6 us
    dot_general x1, matrix products, local_product(): result = jnp.dot(l_strip, b_strip, preferred_element_type=jnp.float32)  26 us
  transfers between devices with their start and end apart: 2, of which 2 were waited for; matrix products, arithmetic and copies ran while one was open for 0% of the time, Pallas kernels for 0%

commit v1 on v0

v1 whole, which is shorter than its diff:
```python
import functools

import jax
import jax.numpy as jnp
from jax import lax
from jax.experimental import pallas as pl
from jax.experimental.pallas import tpu as pltpu
from jax.sharding import PartitionSpec as P

MESH = pl.DeviceIdType.MESH
CHUNK = 256
LEAD = 3


def _body(n_row, n_col, l_ref, b_ref, x_ref, lbuf, bbuf, xst,
          l_recv, l_send, l_loc, b_recv, b_loc, send, x_recv, x_loc):
    row = lax.axis_index("row")
    col = lax.axis_index("col")
    m, n = b_ref.shape
    strip = l_ref.shape[1]
    per_block = m // strip
    n_ch = n // CHUNK
    half = n_ch // 2

    barrier = pltpu.get_barrier_semaphore()
    for d in range(1, n_col):
        pl.semaphore_signal(barrier, inc=1, device_id={"col": lax.rem(col + d, n_col)}, device_id_type=MESH)
    for d in (1, n_row - 1):
        pl.semaphore_signal(barrier, inc=1, device_id={"row": lax.rem(row + d, n_row)}, device_id_type=MESH)

    def cols(ch):
        return pl.ds(pl.multiple_of(ch * CHUNK, CHUNK), CHUNK)

    def strip_cols(j):
        return pl.ds(pl.multiple_of(j * strip, strip), strip)

    def block(q, ch):
        return bbuf.at[ch, pl.ds(q * m, m), :]

    def b_load(q, ch):
        return pltpu.make_async_copy(b_ref.at[:, cols(ch)], block(q, ch), b_loc.at[ch])

    def b_own(q, ch, to, kind):
        return pltpu.make_async_remote_copy(
            src_ref=b_ref.at[:, cols(ch)], dst_ref=block(q, ch), send_sem=send.at[kind, ch],
            recv_sem=b_recv.at[q, ch], device_id={"row": to}, device_id_type=MESH)

    def b_fwd(q, ch, to, kind):
        return pltpu.make_async_remote_copy(
            src_ref=block(q, ch), dst_ref=block(q, ch), send_sem=send.at[kind, ch],
            recv_sem=b_recv.at[q, ch], device_id={"row": to}, device_id_type=MESH)

    def x_back(slot, ch, to):
        return pltpu.make_async_remote_copy(
            src_ref=xst.at[slot], dst_ref=x_ref.at[:, cols(ch)], send_sem=send.at[1, ch],
            recv_sem=x_recv.at[lax.rem(ch, half)], device_id={"row": to}, device_id_type=MESH)

    def x_put(slot, ch):
        return pltpu.make_async_copy(xst.at[slot], x_ref.at[:, cols(ch)], x_loc.at[ch])

    def l_place(s, j):
        return lbuf.at[s, :, strip_cols(j)]

    def l_own(s, d):
        return pltpu.make_async_remote_copy(
            src_ref=l_ref, dst_ref=l_place(s, col), send_sem=l_send.at[0, d],
            recv_sem=l_recv.at[s, col], device_id={"col": lax.rem(col + d, n_col)}, device_id_type=MESH)

    def l_fwd(s, d):
        return pltpu.make_async_remote_copy(
            src_ref=l_place(s, col), dst_ref=l_place(s, col), send_sem=l_send.at[1, d],
            recv_sem=l_recv.at[s, col], device_id={"col": lax.rem(col + d, n_col)}, device_id_type=MESH)

    def l_cross(s, to):
        return pltpu.make_async_remote_copy(
            src_ref=l_ref, dst_ref=l_place(s, col), send_sem=l_send.at[0, 0],
            recv_sem=l_recv.at[s, col], device_id={"row": to}, device_id_type=MESH)

    def l_arrival(s, j):
        return pltpu.make_async_remote_copy(
            src_ref=l_ref, dst_ref=l_place(s, j), send_sem=l_send.at[0, 0],
            recv_sem=l_recv.at[s, j], device_id={"col": lax.rem(col + 1, n_col)}, device_id_type=MESH)

    def l_load(s):
        return pltpu.make_async_copy(l_ref, l_place(s, col), l_loc)

    def each(lo, hi, fn):
        def step(i, carry):
            fn(i)
            return carry
        lax.fori_loop(lo, hi, step, 0)

    def dot(s, depth, ch):
        return jnp.dot(lbuf[s, :, :depth], bbuf[ch, :depth, :], preferred_element_type=jnp.float32).astype(xst.dtype)

    def load_start(q, lo, hi):
        each(lo, hi, lambda ch: b_load(q, ch).start())

    def l_gather_start(s, blocks):
        l_load(s).start()

        @pl.when(col < blocks * per_block)
        def _():
            for d in range(1, n_col):
                l_own(s, d).start()

    def l_gather_wait_own(s, blocks):
        for j in range(blocks * per_block):
            @pl.when(col != j)
            def _():
                l_arrival(s, j).wait_recv()

    def l_gather_drain(s, blocks):
        @pl.when(col < blocks * per_block)
        def _():
            for d in range(1, n_col):
                l_own(s, d).wait_send()


    def row0():
        load_start(0, 0, n_ch)
        pl.semaphore_wait(barrier, n_col + 1)
        for i in range(LEAD):
            b_own(0, i, 1, 0).start()
        for i in range(2):
            b_own(0, half + i, 3, 1).start()
        l_gather_start(0, 1)
        l_load(0).wait()
        l_gather_wait_own(0, 1)

        def step(k):
            b_own(0, half + k, 1, 0).start()

            @pl.when(k + LEAD < half)
            def _():
                b_own(0, k + LEAD, 1, 0).start()

            @pl.when(k + 2 < half)
            def _():
                b_own(0, half + k + 2, 3, 1).start()
            b_fwd(1, half + k, 3, 2).wait_recv()
            b_fwd(1, half + k, 3, 2).start()
            for i in range(2):
                ch = 2 * k + i
                b_load(0, ch).wait()
                xst[ch] = dot(0, m, ch)
                x_put(ch, ch).start()
        each(0, half, step)

        def drain(k):
            b_own(0, k, 1, 0).wait_send()
            b_own(0, half + k, 1, 0).wait_send()
            b_own(0, half + k, 3, 1).wait_send()
            b_fwd(1, half + k, 3, 2).wait_send()
            x_put(k, k).wait()
            x_put(half + k, half + k).wait()
        each(0, half, drain)
        l_gather_drain(0, 1)

    def row1():
        load_start(1, 0, n_ch)
        pl.semaphore_wait(barrier, n_col + 1)
        for i in range(LEAD):
            b_own(1, i, 2, 0).start()
            b_own(1, half + i, 0, 2).start()
        l_gather_start(0, 2)
        l_load(0).wait()
        l_gather_wait_own(0, 2)

        def product(ch):
            b_load(1, ch).wait()
            xst[ch] = dot(0, 2 * m, ch)
            x_put(ch, ch).start()

        def step(k):
            b_fwd(0, k, 2, 1).wait_recv()
            b_fwd(0, k, 2, 1).start()

            @pl.when(k + LEAD < half)
            def _():
                b_own(1, k + LEAD, 2, 0).start()
                b_own(1, half + k + LEAD, 0, 2).start()
            product(k)

            @pl.when(k >= LEAD)
            def _():
                b_fwd(0, half + k - LEAD, 2, 1).wait_recv()
                product(half + k - LEAD)
        each(0, half, step)

        def tail(k):
            b_fwd(0, k, 2, 1).wait_recv()
            product(k)
        each(n_ch - LEAD, n_ch, tail)

        def drain(k):
            b_own(1, k, 2, 0).wait_send()
            b_own(1, half + k, 0, 2).wait_send()
            b_fwd(0, k, 2, 1).wait_send()
            x_put(k, k).wait()
            x_put(half + k, half + k).wait()
        each(0, half, drain)
        l_gather_drain(0, 2)

    def lower(p):
        o = 5 - p
        s, so = p - 2, o - 2
        base, other = s * half, so * half
        load_start(p, base, base + half)
        pl.semaphore_wait(barrier, n_col + 1)

        @pl.when(col < (p + 1) * per_block)
        def _():
            l_cross(s, o).start()
        l_gather_start(s, p + 1)
        each(other, other + half, lambda ch: b_own(p, ch, o, 0).start())

        @pl.when(col < (o + 1) * per_block)
        def _():
            l_arrival(so, col).wait_recv()
            for d in range(1, n_col):
                l_fwd(so, d).start()
        l_load(s).wait()
        l_gather_wait_own(s, p + 1)
        l_gather_wait_own(so, o + 1)

        def step(ch):
            for q in range(4):
                if q != p:
                    b_fwd(q, ch, o, 0).wait_recv()
            b_load(p, ch).wait()
            away = 2 * (ch - base)
            xst[away] = dot(so, (o + 1) * m, ch)
            x_back(away, ch, o).start()
            xst[away + 1] = dot(s, (p + 1) * m, ch)
            x_put(away + 1, ch).start()
        each(base, base + half, step)

        def drain(k):
            b_own(p, other + k, o, 0).wait_send()
            x_back(2 * k, base + k, o).wait_send()
            x_put(2 * k + 1, base + k).wait()
            x_back(2 * k, other + k, o).wait_recv()
        each(0, half, drain)
        l_gather_drain(s, p + 1)

        @pl.when(col < (p + 1) * per_block)
        def _():
            l_cross(s, o).wait_send()

        @pl.when(col < (o + 1) * per_block)
        def _():
            for d in range(1, n_col):
                l_fwd(so, d).wait_send()

    pl.when(row == 0)(row0)
    pl.when(row == 1)(row1)
    pl.when(row == 2)(functools.partial(lower, 2))
    pl.when(row == 3)(functools.partial(lower, 3))


def solution(mesh):
    spec = P(("batch", "row"), "col")
    n_row, n_col = mesh.shape["row"], mesh.shape["col"]
    assert n_row == 4

    def local(l_block, b_block):
        m, n = b_block.shape
        k = n_row * m
        n_ch = n // CHUNK
        dma = pltpu.SemaphoreType.DMA
        return pl.pallas_call(
            functools.partial(_body, n_row, n_col),
            out_shape=jax.ShapeDtypeStruct((m, n), b_block.dtype),
            in_specs=[pl.BlockSpec(memory_space=pl.ANY)] * 2,
            out_specs=pl.BlockSpec(memory_space=pl.ANY),
            scratch_shapes=[
                pltpu.VMEM((2, m, k), l_block.dtype),
                pltpu.VMEM((n_ch, k, CHUNK), b_block.dtype),
                pltpu.VMEM((n_ch, m, CHUNK), b_block.dtype),
                dma((2, n_col)),
                dma((2, n_col)),
                dma(()),
                dma((n_row, n_ch)),
                dma((n_ch,)),
                dma((3, n_ch)),
                dma((n_ch // 2,)),
                dma((n_ch,)),
            ],
            compiler_params=pltpu.CompilerParams(
                collective_id=0, has_side_effects=True, vmem_limit_bytes=60 * 1024 * 1024),
            name="tri_ring",
        )(l_block, b_block)

    return jax.shard_map(local, mesh=mesh, in_specs=(spec, spec), out_specs=spec, check_vma=False)
```

time: 364 us -> 212 us (0.58)
  the two profiles are of different devices: /device:TPU:112 before, /device:TPU:117 now
where the time goes in v1:
time: 212 us
  Pallas kernels  204 us (96%)
  local copies, waits for them, and re-layouts  7.77 us (4%)
    pallas_call x1, Pallas kernels, local(): pl.pallas_call(functools.partial(_body, n_row, n_col), out_shape=jax.Shap...  204 us
    unnamed x1, local copies, waits for them, and re-layouts  7.77 us

profile of v1, /device:TPU:117, one launch (start us, length us, event | category | flops | bytes accessed | tf_op | source)
XLA Modules:
  0.0 211.5 jit_solution(4278076915970240906)
XLA Ops:
  0.0 203.7 %tri_ring.1 = bf16[512,8192]{1,0:T(8,128)(2,1)} custom-call(bf16[512,256]{1,0:T(8,128)(2,1)} %l_ref.1, bf16[512,8192]{1,0:T(8,128)(2,1)} %b_ref.1), custom_call_target="tpu_custom_call" | custom-call | tf_op jit(solution)/shard_map/tri_ring/pallas_call | solution.py:272
  203.8 7.8 %copy.4 = bf16[512,8192]{1,0:T(8,128)(2,1)} copy(bf16[512,8192]{1,0:T(8,128)(2,1)} %tri_ring.1) | data formatting | bytes 16777216

commit v2 on v1

--- a/solution.py
+++ b/solution.py
@@ -10,10 +10,12 @@
 MESH = pl.DeviceIdType.MESH
 CHUNK = 256
 LEAD = 3
+LAG = 4
+STORES = 8
 
 
 def _body(n_row, n_col, l_ref, b_ref, x_ref, lbuf, bbuf, xst,
-          l_recv, l_send, l_loc, b_recv, b_loc, send, x_recv, x_loc):
+          l_recv, l_send, l_loc, b_recv, b_loc, send, x_recv):
     row = lax.axis_index("row")
     col = lax.axis_index("col")
     m, n = b_ref.shape
@@ -54,9 +56,6 @@
         return pltpu.make_async_remote_copy(
             src_ref=xst.at[slot], dst_ref=x_ref.at[:, cols(ch)], send_sem=send.at[1, ch],
             recv_sem=x_recv.at[lax.rem(ch, half)], device_id={"row": to}, device_id_type=MESH)
-
-    def x_put(slot, ch):
-        return pltpu.make_async_copy(xst.at[slot], x_ref.at[:, cols(ch)], x_loc.at[ch])
 
     def l_place(s, j):
         return lbuf.at[s, :, strip_cols(j)]
@@ -125,8 +124,10 @@
         for i in range(2):
             b_own(0, half + i, 3, 1).start()
         l_gather_start(0, 1)
-        l_load(0).wait()
-        l_gather_wait_own(0, 1)
+
+        def product(ch):
+            b_load(0, ch).wait()
+            x_ref[:, cols(ch)] = dot(0, m, ch)
 
         def step(k):
             b_own(0, half + k, 1, 0).start()
@@ -140,11 +141,16 @@
                 b_own(0, half + k + 2, 3, 1).start()
             b_fwd(1, half + k, 3, 2).wait_recv()
             b_fwd(1, half + k, 3, 2).start()
-            for i in range(2):
-                ch = 2 * k + i
-                b_load(0, ch).wait()
-                xst[ch] = dot(0, m, ch)
-                x_put(ch, ch).start()
+
+            @pl.when(k == LAG)
+            def _():
+                l_load(0).wait()
+                l_gather_wait_own(0, 1)
+
+            @pl.when(k >= LAG)
+            def _():
+                done = (k - LAG) * n_ch // (half - LAG)
+                each(done, (k + 1 - LAG) * n_ch // (half - LAG), product)
         each(0, half, step)
 
         def drain(k):
@@ -152,8 +158,6 @@
             b_own(0, half + k, 1, 0).wait_send()
             b_own(0, half + k, 3, 1).wait_send()
             b_fwd(1, half + k, 3, 2).wait_send()
-            x_put(k, k).wait()
-            x_put(half + k, half + k).wait()
         each(0, half, drain)
         l_gather_drain(0, 1)
 
@@ -164,13 +168,20 @@
             b_own(1, i, 2, 0).start()
             b_own(1, half + i, 0, 2).start()
         l_gather_start(0, 2)
-        l_load(0).wait()
-        l_gather_wait_own(0, 2)
 
         def product(ch):
             b_load(1, ch).wait()
-            xst[ch] = dot(0, 2 * m, ch)
-            x_put(ch, ch).start()
+            x_ref[:, cols(ch)] = dot(0, 2 * m, ch)
+
+        def late_product(ch):
+            b_fwd(0, ch, 2, 1).wait_recv()
+            product(ch)
+
+        def first_done(k):
+            return jnp.clip(2 * (k + 1 - LAG), 0, k + 1)
+
+        def second_done(k):
+            return jnp.clip(2 * (k + 1 - LAG), 0, jnp.maximum(k + 1 - LEAD, 0))
 
         def step(k):
             b_fwd(0, k, 2, 1).wait_recv()
@@ -180,25 +191,20 @@
             def _():
                 b_own(1, k + LEAD, 2, 0).start()
                 b_own(1, half + k + LEAD, 0, 2).start()
-            product(k)
-
-            @pl.when(k >= LEAD)
-            def _():
-                b_fwd(0, half + k - LEAD, 2, 1).wait_recv()
-                product(half + k - LEAD)
+
+            @pl.when(k == LAG)
+            def _():
+                l_load(0).wait()
+                l_gather_wait_own(0, 2)
+            each(first_done(k - 1), first_done(k), product)
+            each(half + second_done(k - 1), half + second_done(k), late_product)
         each(0, half, step)
-
-        def tail(k):
-            b_fwd(0, k, 2, 1).wait_recv()
-            product(k)
-        each(n_ch - LEAD, n_ch, tail)
+        each(n_ch - LEAD, n_ch, late_product)
 
         def drain(k):
             b_own(1, k, 2, 0).wait_send()
             b_own(1, half + k, 0, 2).wait_send()
             b_fwd(0, k, 2, 1).wait_send()
-            x_put(k, k).wait()
-            x_put(half + k, half + k).wait()
         each(0, half, drain)
         l_gather_drain(0, 2)
 
@@ -229,18 +235,16 @@
                 if q != p:
                     b_fwd(q, ch, o, 0).wait_recv()
             b_load(p, ch).wait()
-            away = 2 * (ch - base)
+            away = ch - base
             xst[away] = dot(so, (o + 1) * m, ch)
             x_back(away, ch, o).start()
-            xst[away + 1] = dot(s, (p + 1) * m, ch)
-            x_put(away + 1, ch).start()
+            x_ref[:, cols(ch)] = dot(s, (p + 1) * m, ch)
         each(base, base + half, step)
 
         def drain(k):
             b_own(p, other + k, o, 0).wait_send()
-            x_back(2 * k, base + k, o).wait_send()
-            x_put(2 * k + 1, base + k).wait()
-            x_back(2 * k, other + k, o).wait_recv()
+            x_back(k, base + k, o).wait_send()
+            x_back(k, other + k, o).wait_recv()
         each(0, half, drain)
         l_gather_drain(s, p + 1)
 
@@ -257,6 +261,16 @@
     pl.when(row == 1)(row1)
     pl.when(row == 2)(functools.partial(lower, 2))
     pl.when(row == 3)(functools.partial(lower, 3))
+
+
+def _store_body(v_ref, x_ref, sem):
+    rows = v_ref.shape[0] // STORES
+    copies = [pltpu.make_async_copy(v_ref.at[pl.ds(i * rows, rows), :], x_ref.at[pl.ds(i * rows, rows), :], sem.at[i])
+              for i in range(STORES)]
+    for copy in copies:
+        copy.start()
+    for copy in copies:
+        copy.wait()
 
 
 def solution(mesh):
@@ -269,15 +283,15 @@
         k = n_row * m
         n_ch = n // CHUNK
         dma = pltpu.SemaphoreType.DMA
-        return pl.pallas_call(
+        x = pl.pallas_call(
             functools.partial(_body, n_row, n_col),
-            out_shape=jax.ShapeDtypeStruct((m, n), b_block.dtype),
+            out_shape=pltpu.VMEM((m, n), b_block.dtype),
             in_specs=[pl.BlockSpec(memory_space=pl.ANY)] * 2,
-            out_specs=pl.BlockSpec(memory_space=pl.ANY),
+            out_specs=pl.BlockSpec(memory_space=pltpu.VMEM),
             scratch_shapes=[
                 pltpu.VMEM((2, m, k), l_block.dtype),
                 pltpu.VMEM((n_ch, k, CHUNK), b_block.dtype),
-                pltpu.VMEM((n_ch, m, CHUNK), b_block.dtype),
+                pltpu.VMEM((n_ch // 2, m, CHUNK), b_block.dtype),
                 dma((2, n_col)),
                 dma((2, n_col)),
                 dma(()),
@@ -285,11 +299,19 @@
                 dma((n_ch,)),
                 dma((3, n_ch)),
                 dma((n_ch // 2,)),
-                dma((n_ch,)),
             ],
             compiler_params=pltpu.CompilerParams(
-                collective_id=0, has_side_effects=True, vmem_limit_bytes=60 * 1024 * 1024),
+                collective_id=0, has_side_effects=True, vmem_limit_bytes=50 * 1024 * 1024),
             name="tri_ring",
         )(l_block, b_block)
+        return pl.pallas_call(
+            _store_body,
+            out_shape=jax.ShapeDtypeStruct((m, n), b_block.dtype),
+            in_specs=[pl.BlockSpec(memory_space=pltpu.VMEM)],
+            out_specs=pl.BlockSpec(memory_space=pl.ANY),
+            scratch_shapes=[dma((STORES,))],
+            compiler_params=pltpu.CompilerParams(vmem_limit_bytes=1024 * 1024),
+            name="tri_store",
+        )(pltpu.with_memory_space_constraint(x, pltpu.VMEM))
 
     return jax.shard_map(local, mesh=mesh, in_specs=(spec, spec), out_specs=spec, check_vma=False)

time: 212 us -> 198 us (0.934)
  the two profiles are of different devices: /device:TPU:117 before, /device:TPU:112 now
where the time goes in v2:
time: 198 us
  Pallas kernels  198 us (100%)
    pallas_call x1, Pallas kernels, local(): pl.pallas_call(functools.partial(_body, n_row, n_col), out_shape=pltpu.VM...  195 us

profile of v2, /device:TPU:112, one launch (start us, length us, event | category | flops | bytes accessed | tf_op | source)
XLA Modules:
  0.0 197.9 jit_solution(13308086195969756749)
XLA Ops:
  0.0 194.5 %tri_ring.1.v_ref = bf16[512,8192]{1,0:T(8,128)(2,1)S(1)} custom-call(bf16[512,256]{1,0:T(8,128)(2,1)} %l_ref.1, bf16[512,8192]{1,0:T(8,128)(2,1)} %b_ref.1), custom_call_target="tpu_custom_call" | custom-call | tf_op jit(solution)/shard_map/tri_ring/pallas_call | solution.py:286
  194.5 3.4 %tri_store.1 = bf16[512,8192]{1,0:T(8,128)(2,1)} custom-call(bf16[512,8192]{1,0:T(8,128)(2,1)S(1)} %tri_ring.1.v_ref), custom_call_target="tpu_custom_call" | custom-call | tf_op jit(solution)/shard_map/tri_store/pallas_call | solution.py:307

commit v3 on v2

--- a/solution.py
+++ b/solution.py
@@ -9,8 +9,12 @@
 
 MESH = pl.DeviceIdType.MESH
 CHUNK = 256
+DIRECT = 2
 LEAD = 3
+LEAD_A = 5
+RELAY = 2
 LAG = 4
+SPECIAL = 9
 STORES = 8
 
 
@@ -22,7 +26,8 @@
     strip = l_ref.shape[1]
     per_block = m // strip
     n_ch = n // CHUNK
-    half = n_ch // 2
+    half = (n_ch - DIRECT) // 2
+    top = 2 * half
 
     barrier = pltpu.get_barrier_semaphore()
     for d in range(1, n_col):
@@ -55,7 +60,7 @@
     def x_back(slot, ch, to):
         return pltpu.make_async_remote_copy(
             src_ref=xst.at[slot], dst_ref=x_ref.at[:, cols(ch)], send_sem=send.at[1, ch],
-            recv_sem=x_recv.at[lax.rem(ch, half)], device_id={"row": to}, device_id_type=MESH)
+            recv_sem=x_recv.at[ch], device_id={"row": to}, device_id_type=MESH)
 
     def l_place(s, j):
         return lbuf.at[s, :, strip_cols(j)]
@@ -70,9 +75,9 @@
             src_ref=l_place(s, col), dst_ref=l_place(s, col), send_sem=l_send.at[1, d],
             recv_sem=l_recv.at[s, col], device_id={"col": lax.rem(col + d, n_col)}, device_id_type=MESH)
 
-    def l_cross(s, to):
-        return pltpu.make_async_remote_copy(
-            src_ref=l_ref, dst_ref=l_place(s, col), send_sem=l_send.at[0, 0],
+    def l_cross(s, to, kind):
+        return pltpu.make_async_remote_copy(
+            src_ref=l_ref, dst_ref=l_place(s, col), send_sem=l_send.at[kind, 0],
             recv_sem=l_recv.at[s, col], device_id={"row": to}, device_id_type=MESH)
 
     def l_arrival(s, j):
@@ -95,62 +100,99 @@
     def load_start(q, lo, hi):
         each(lo, hi, lambda ch: b_load(q, ch).start())
 
+
+    def holds(blocks):
+        return col < blocks * per_block
+
     def l_gather_start(s, blocks):
         l_load(s).start()
 
-        @pl.when(col < blocks * per_block)
+        @pl.when(holds(blocks))
         def _():
             for d in range(1, n_col):
                 l_own(s, d).start()
 
-    def l_gather_wait_own(s, blocks):
+    def l_gather_wait(s, blocks):
         for j in range(blocks * per_block):
             @pl.when(col != j)
             def _():
                 l_arrival(s, j).wait_recv()
 
     def l_gather_drain(s, blocks):
-        @pl.when(col < blocks * per_block)
+        @pl.when(holds(blocks))
         def _():
             for d in range(1, n_col):
                 l_own(s, d).wait_send()
+
+    def l_relay_start(s, blocks):
+        @pl.when(holds(blocks))
+        def _():
+            l_arrival(s, col).wait_recv()
+            for d in range(1, n_col):
+                l_fwd(s, d).start()
+
+    def l_relay_drain(s, blocks):
+        @pl.when(holds(blocks))
+        def _():
+            for d in range(1, n_col):
+                l_fwd(s, d).wait_send()
 
 
     def row0():
         load_start(0, 0, n_ch)
         pl.semaphore_wait(barrier, n_col + 1)
+        for i in range(LEAD_A):
+            b_own(0, i, 1, 0).start()
         for i in range(LEAD):
-            b_own(0, i, 1, 0).start()
-        for i in range(2):
             b_own(0, half + i, 3, 1).start()
+        each(top, n_ch, lambda ch: b_own(0, ch, 1, 0).start())
         l_gather_start(0, 1)
 
         def product(ch):
             b_load(0, ch).wait()
             x_ref[:, cols(ch)] = dot(0, m, ch)
 
+        def special(ch):
+            product(ch)
+            for q in range(1, 4):
+                b_fwd(q, ch, 1, 0).wait_recv()
+            xst[ch - top] = dot(1, 4 * m, ch)
+
         def step(k):
             b_own(0, half + k, 1, 0).start()
 
+            @pl.when(k + LEAD_A < half)
+            def _():
+                b_own(0, k + LEAD_A, 1, 0).start()
+
             @pl.when(k + LEAD < half)
             def _():
-                b_own(0, k + LEAD, 1, 0).start()
-
-            @pl.when(k + 2 < half)
-            def _():
-                b_own(0, half + k + 2, 3, 1).start()
+                b_own(0, half + k + LEAD, 3, 1).start()
             b_fwd(1, half + k, 3, 2).wait_recv()
             b_fwd(1, half + k, 3, 2).start()
 
+            @pl.when(k == half - 1)
+            def _():
+                each(top, n_ch, lambda ch: x_back(ch - top, ch, 3).start())
+
+            @pl.when(k == RELAY)
+            def _():
+                l_relay_start(1, 4)
+
             @pl.when(k == LAG)
             def _():
                 l_load(0).wait()
-                l_gather_wait_own(0, 1)
+                l_gather_wait(0, 1)
 
             @pl.when(k >= LAG)
             def _():
-                done = (k - LAG) * n_ch // (half - LAG)
-                each(done, (k + 1 - LAG) * n_ch // (half - LAG), product)
+                done = (k - LAG) * top // (half - LAG)
+                each(done, (k + 1 - LAG) * top // (half - LAG), product)
+
+            @pl.when(k == SPECIAL)
+            def _():
+                l_gather_wait(1, 4)
+                each(top, n_ch, special)
         each(0, half, step)
 
         def drain(k):
@@ -159,7 +201,13 @@
             b_own(0, half + k, 3, 1).wait_send()
             b_fwd(1, half + k, 3, 2).wait_send()
         each(0, half, drain)
+
+        def drain_special(ch):
+            b_own(0, ch, 1, 0).wait_send()
+            x_back(ch - top, ch, 3).wait_send()
+        each(top, n_ch, drain_special)
         l_gather_drain(0, 1)
+        l_relay_drain(1, 4)
 
     def row1():
         load_start(1, 0, n_ch)
@@ -177,11 +225,20 @@
             b_fwd(0, ch, 2, 1).wait_recv()
             product(ch)
 
+        def special(ch):
+            late_product(ch)
+            xst[ch - top] = dot(1, 3 * m, ch)
+
+        def special_relay(ch):
+            b_own(1, ch, 0, 2).start()
+            b_fwd(2, ch, 0, 0).wait_recv()
+            b_fwd(2, ch, 0, 0).start()
+
         def first_done(k):
             return jnp.clip(2 * (k + 1 - LAG), 0, k + 1)
 
         def second_done(k):
-            return jnp.clip(2 * (k + 1 - LAG), 0, jnp.maximum(k + 1 - LEAD, 0))
+            return jnp.clip(2 * (k + 1 - LAG), 0, jnp.maximum(k + 1 - LEAD_A, 0))
 
         def step(k):
             b_fwd(0, k, 2, 1).wait_recv()
@@ -192,43 +249,61 @@
                 b_own(1, k + LEAD, 2, 0).start()
                 b_own(1, half + k + LEAD, 0, 2).start()
 
+            @pl.when(k == half - 1)
+            def _():
+                each(top, n_ch, lambda ch: x_back(ch - top, ch, 2).start())
+
+            @pl.when(k == RELAY)
+            def _():
+                each(top, n_ch, special_relay)
+                l_relay_start(1, 3)
+
             @pl.when(k == LAG)
             def _():
                 l_load(0).wait()
-                l_gather_wait_own(0, 2)
+                l_gather_wait(0, 2)
             each(first_done(k - 1), first_done(k), product)
             each(half + second_done(k - 1), half + second_done(k), late_product)
+
+            @pl.when(k == SPECIAL)
+            def _():
+                l_gather_wait(1, 3)
+                each(top, n_ch, special)
         each(0, half, step)
-        each(n_ch - LEAD, n_ch, late_product)
+        each(top - LEAD_A, top, late_product)
 
         def drain(k):
             b_own(1, k, 2, 0).wait_send()
             b_own(1, half + k, 0, 2).wait_send()
             b_fwd(0, k, 2, 1).wait_send()
         each(0, half, drain)
+
+        def drain_special(ch):
+            b_own(1, ch, 0, 2).wait_send()
+            b_fwd(2, ch, 0, 0).wait_send()
+            x_back(ch - top, ch, 2).wait_send()
+        each(top, n_ch, drain_special)
         l_gather_drain(0, 2)
+        l_relay_drain(1, 3)
 
     def lower(p):
-        o = 5 - p
+        o, u = 5 - p, 1 if p == 2 else 0
         s, so = p - 2, o - 2
         base, other = s * half, so * half
         load_start(p, base, base + half)
         pl.semaphore_wait(barrier, n_col + 1)
 
-        @pl.when(col < (p + 1) * per_block)
-        def _():
-            l_cross(s, o).start()
+        @pl.when(holds(p + 1))
+        def _():
+            l_cross(s, o, 0).start()
+            l_cross(1, u, 1).start()
         l_gather_start(s, p + 1)
+        each(top, n_ch, lambda ch: b_own(p, ch, u, 0).start())
         each(other, other + half, lambda ch: b_own(p, ch, o, 0).start())
-
-        @pl.when(col < (o + 1) * per_block)
-        def _():
-            l_arrival(so, col).wait_recv()
-            for d in range(1, n_col):
-                l_fwd(so, d).start()
+        l_relay_start(so, o + 1)
         l_load(s).wait()
-        l_gather_wait_own(s, p + 1)
-        l_gather_wait_own(so, o + 1)
+        l_gather_wait(s, p + 1)
+        l_gather_wait(so, o + 1)
 
         def step(ch):
             for q in range(4):
@@ -246,16 +321,18 @@
             x_back(k, base + k, o).wait_send()
             x_back(k, other + k, o).wait_recv()
         each(0, half, drain)
+
+        def drain_special(ch):
+            b_own(p, ch, u, 0).wait_send()
+            x_back(ch - top, ch, u).wait_recv()
+        each(top, n_ch, drain_special)
         l_gather_drain(s, p + 1)
-
-        @pl.when(col < (p + 1) * per_block)
-        def _():
-            l_cross(s, o).wait_send()
-
-        @pl.when(col < (o + 1) * per_block)
-        def _():
-            for d in range(1, n_col):
-                l_fwd(so, d).wait_send()
+        l_relay_drain(so, o + 1)
+
+        @pl.when(holds(p + 1))
+        def _():
+            l_cross(s, o, 0).wait_send()
+            l_cross(1, u, 1).wait_send()
 
     pl.when(row == 0)(row0)
     pl.when(row == 1)(row1)
@@ -291,14 +368,14 @@
             scratch_shapes=[
                 pltpu.VMEM((2, m, k), l_block.dtype),
                 pltpu.VMEM((n_ch, k, CHUNK), b_block.dtype),
-                pltpu.VMEM((n_ch // 2, m, CHUNK), b_block.dtype),
+                pltpu.VMEM(((n_ch - DIRECT) // 2, m, CHUNK), b_block.dtype),
                 dma((2, n_col)),
                 dma((2, n_col)),
                 dma(()),
                 dma((n_row, n_ch)),
                 dma((n_ch,)),
                 dma((3, n_ch)),
-                dma((n_ch // 2,)),
+                dma((n_ch,)),
             ],
             compiler_params=pltpu.CompilerParams(
                 collective_id=0, has_side_effects=True, vmem_limit_bytes=50 * 1024 * 1024),

time: 198 us -> 192 us (0.970)
  Pallas kernels: 198 us -> 190 us
    pallas_call x1, Pallas kernels: 195 us -> 187 us  [local(): pl.pallas_call(functools.partial(_body, n_row, n_col), out_shape=pltpu.VM...]
where the time goes in v3:
time: 192 us; the launch traced here: 190 us
  Pallas kernels  190 us (99%)
    pallas_call x1, Pallas kernels, local(): pl.pallas_call(functools.partial(_body, n_row, n_col), out_shape=pltpu.VM...  187 us

profile of v3, /device:TPU:112, one launch (start us, length us, event | category | flops | bytes accessed | tf_op | source)
XLA Modules:
  0.0 190.2 jit_solution(15252996190833919291)
XLA Ops:
  0.0 186.8 %tri_ring.1.v_ref = bf16[512,8192]{1,0:T(8,128)(2,1)S(1)} custom-call(bf16[512,256]{1,0:T(8,128)(2,1)} %l_ref.1, bf16[512,8192]{1,0:T(8,128)(2,1)} %b_ref.1), custom_call_target="tpu_custom_call" | custom-call | tf_op jit(solution)/shard_map/tri_ring/pallas_call | solution.py:363
  186.8 3.4 %tri_store.1 = bf16[512,8192]{1,0:T(8,128)(2,1)} custom-call(bf16[512,8192]{1,0:T(8,128)(2,1)S(1)} %tri_ring.1.v_ref), custom_call_target="tpu_custom_call" | custom-call | tf_op jit(solution)/shard_map/tri_store/pallas_call | solution.py:384

commit v4 on v3

--- a/solution.py
+++ b/solution.py
@@ -8,13 +8,13 @@
 from jax.sharding import PartitionSpec as P
 
 MESH = pl.DeviceIdType.MESH
-CHUNK = 256
+CHUNK = 512
 DIRECT = 2
-LEAD = 3
-LEAD_A = 5
-RELAY = 2
-LAG = 4
-SPECIAL = 9
+LEAD = 2
+LEAD_A = 3
+RELAY = 1
+LAG = 3
+SPECIAL = 5
 STORES = 8
 
 
@@ -30,10 +30,10 @@
     top = 2 * half
 
     barrier = pltpu.get_barrier_semaphore()
+    for d in (1, n_row - 1):
+        pl.semaphore_signal(barrier, inc=1, device_id={"row": lax.rem(row + d, n_row)}, device_id_type=MESH)
     for d in range(1, n_col):
         pl.semaphore_signal(barrier, inc=1, device_id={"col": lax.rem(col + d, n_col)}, device_id_type=MESH)
-    for d in (1, n_row - 1):
-        pl.semaphore_signal(barrier, inc=1, device_id={"row": lax.rem(row + d, n_row)}, device_id_type=MESH)
 
     def cols(ch):
         return pl.ds(pl.multiple_of(ch * CHUNK, CHUNK), CHUNK)

time: 192 us -> 191 us (level)
  no operation moved by 1% of the time
where the time goes in v4:
time: 191 us; the launch traced here: 190 us
  Pallas kernels  190 us (99%)
    pallas_call x1, Pallas kernels, local(): pl.pallas_call(functools.partial(_body, n_row, n_col), out_shape=pltpu.VM...  186 us

profile of v4, /device:TPU:112, one launch (start us, length us, event | category | flops | bytes accessed | tf_op | source)
XLA Modules:
  0.0 189.6 jit_solution(4991711981050702863)
XLA Ops:
  0.0 186.2 %tri_ring.1.v_ref = bf16[512,8192]{1,0:T(8,128)(2,1)S(1)} custom-call(bf16[512,256]{1,0:T(8,128)(2,1)} %l_ref.1, bf16[512,8192]{1,0:T(8,128)(2,1)} %b_ref.1), custom_call_target="tpu_custom_call" | custom-call | tf_op jit(solution)/shard_map/tri_ring/pallas_call | solution.py:363
  186.2 3.4 %tri_store.1 = bf16[512,8192]{1,0:T(8,128)(2,1)} custom-call(bf16[512,8192]{1,0:T(8,128)(2,1)S(1)} %tri_ring.1.v_ref), custom_call_target="tpu_custom_call" | custom-call | tf_op jit(solution)/shard_map/tri_store/pallas_call | solution.py:384

commit v5 on v0

v5 whole, which is shorter than its diff:
```python
import functools

import jax
import jax.numpy as jnp
from jax import lax
from jax.experimental import pallas as pl
from jax.experimental.pallas import tpu as pltpu
from jax.sharding import PartitionSpec as P

MESH = pl.DeviceIdType.MESH
STEP = 256
STORES = 8


def _pieces(start, widths, index):
    out = []
    for w in widths:
        out.append((start, w, index))
        start, index = start + w, index + 1
    return out


def _body(n_row, n_col, l_ref, b_ref, x_ref, lbuf, bbuf, xst,
          l_recv, l_cross_recv, l_send, l_loc, b_recv, b_loc, send, x_recv, ready, seen, go):
    row = lax.axis_index("row")
    col = lax.axis_index("col")
    m, n = b_ref.shape
    strip = l_ref.shape[1]
    per_block = m // strip
    unit = n // 8
    part = [unit, unit, unit, unit // 2]
    half = sum(part)
    top = 2 * half
    back = unit // 2
    n_back = half // back

    first = _pieces(0, part, 0)
    second = _pieces(half, part, 4)
    second_fine = _pieces(half, part[:3] + [unit // 4] * 2, 4)
    direct = (top, unit, 9)

    barrier = pltpu.get_barrier_semaphore()

    def to_row(sem, r):
        pl.semaphore_signal(sem, inc=1, device_id={"row": r}, device_id_type=MESH)

    def to_peers(sem):
        for d in range(1, n_col):
            pl.semaphore_signal(sem, inc=1, device_id={"col": lax.rem(col + d, n_col)}, device_id_type=MESH)

    def enter_upper(twin, below):
        to_row(barrier, twin)
        to_row(barrier, below)
        to_peers(barrier)
        pl.semaphore_wait(barrier, n_col)

    def await_below():
        pl.semaphore_wait(ready, 1)

    def release_below(twin, below):
        to_row(seen, twin)
        to_peers(seen)
        pl.semaphore_wait(seen, n_col)
        to_row(go, below)

    def enter_lower(above):
        pl.semaphore_wait(barrier, 1)
        to_row(ready, above)

    def all_bytes(ref, sem):
        pltpu.make_async_copy(ref, ref, sem).wait()

    def strip_cols(j):
        return pl.ds(pl.multiple_of(j * strip, strip), strip)

    def block(q, start, w):
        return bbuf.at[pl.ds(q * m, m), pl.ds(start, w)]

    def b_load(q, start, w):
        return pltpu.make_async_copy(b_ref.at[:, pl.ds(start, w)], block(q, start, w), b_loc)

    def b_own(q, piece, to, slot=None):
        start, w, i = piece
        return pltpu.make_async_remote_copy(
            src_ref=b_ref.at[:, pl.ds(start, w)], dst_ref=block(q, start, w), send_sem=send,
            recv_sem=b_recv.at[i if slot is None else slot], device_id={"row": to}, device_id_type=MESH)

    def b_fwd(q, piece, to):
        start, w, i = piece
        return pltpu.make_async_remote_copy(
            src_ref=block(q, start, w), dst_ref=block(q, start, w), send_sem=send,
            recv_sem=b_recv.at[i], device_id={"row": to}, device_id_type=MESH)

    def b_arrive(piece, blocks=1, slot=None):
        start, w, i = piece
        all_bytes(bbuf.at[pl.ds(0, blocks * m), pl.ds(start, w)], b_recv.at[i if slot is None else slot])

    def x_back(base, t, to):
        return pltpu.make_async_remote_copy(
            src_ref=xst.at[:, pl.ds(pl.multiple_of(t * back, back), back)],
            dst_ref=x_ref.at[:, pl.ds(pl.multiple_of(base + t * back, back), back)],
            send_sem=send, recv_sem=x_recv, device_id={"row": to}, device_id_type=MESH)

    def x_direct(to):
        return pltpu.make_async_remote_copy(
            src_ref=xst.at[:, pl.ds(0, unit)], dst_ref=x_ref.at[:, pl.ds(top, unit)],
            send_sem=send, recv_sem=x_recv, device_id={"row": to}, device_id_type=MESH)

    def sent(halves):
        all_bytes(bbuf.at[:, pl.ds(0, halves * unit // 8)], send)

    def l_place(s, j):
        return lbuf.at[s, :, strip_cols(j)]

    def l_own(s, d):
        return pltpu.make_async_remote_copy(
            src_ref=l_ref, dst_ref=l_place(s, col), send_sem=l_send.at[0],
            recv_sem=l_recv.at[s], device_id={"col": lax.rem(col + d, n_col)}, device_id_type=MESH)

    def l_fwd(s, d):
        return pltpu.make_async_remote_copy(
            src_ref=l_place(s, col), dst_ref=l_place(s, col), send_sem=l_send.at[1],
            recv_sem=l_recv.at[s], device_id={"col": lax.rem(col + d, n_col)}, device_id_type=MESH)

    def l_cross(s, to):
        return pltpu.make_async_remote_copy(
            src_ref=l_ref, dst_ref=l_place(s, col), send_sem=l_send.at[0],
            recv_sem=l_cross_recv, device_id={"row": to}, device_id_type=MESH)

    def l_load(s):
        return pltpu.make_async_copy(l_ref, l_place(s, col), l_loc)

    def each(lo, hi, fn):
        def step(i, carry):
            fn(i)
            return carry
        lax.fori_loop(lo, hi, step, 0)

    def multiply(s, depth, out, shift, start, w):
        def step(i):
            c = pl.multiple_of(start + i * STEP, STEP)
            product = jnp.dot(lbuf[s, :, :depth], bbuf[:depth, pl.ds(c, STEP)], preferred_element_type=jnp.float32)
            out[:, pl.ds(pl.multiple_of(c - shift, STEP), STEP)] = product.astype(out.dtype)
        each(0, w // STEP, step)


    def holds(blocks):
        return col < blocks * per_block

    def l_gather_start(s, blocks):
        l_load(s).start()

        @pl.when(holds(blocks))
        def _():
            for d in range(1, n_col):
                l_own(s, d).start()

    def l_gather_wait(s, blocks):
        count = blocks * per_block

        @pl.when(holds(blocks))
        def _():
            all_bytes(lbuf.at[s, :, pl.ds(0, (count - 1) * strip)], l_recv.at[s])

        @pl.when(jnp.logical_not(holds(blocks)))
        def _():
            all_bytes(lbuf.at[s, :, pl.ds(0, count * strip)], l_recv.at[s])

    def l_gather_drain(blocks, crossed):
        @pl.when(holds(blocks))
        def _():
            all_bytes(lbuf.at[:, :, pl.ds(0, (n_col - 1 + crossed) * strip // 2)], l_send.at[0])

    def l_relay_start(s, blocks):
        @pl.when(holds(blocks))
        def _():
            all_bytes(l_place(s, col), l_cross_recv)
            for d in range(1, n_col):
                l_fwd(s, d).start()

    def l_relay_drain(blocks):
        @pl.when(holds(blocks))
        def _():
            all_bytes(lbuf.at[0, :, pl.ds(0, (n_col - 1) * strip)], l_send.at[1])

    def row0():
        enter_upper(1, 3)
        for piece in first[:2] + [direct] + first[2:] + second_fine:
            b_own(0, piece, 1).start()
        await_below()
        for piece in second[:2]:
            b_own(0, piece, 3).start()
        b_load(0, 0, n).start()
        release_below(1, 3)
        l_gather_start(0, 1)
        for piece in second[:2]:
            b_arrive(piece)
            b_fwd(1, piece, 3).start()
        b_own(0, second[2], 3).start()
        l_relay_start(1, 4)
        l_load(0).wait()
        l_gather_wait(0, 1)
        b_load(0, 0, n).wait()
        multiply(0, m, x_ref, 0, 0, half)
        b_arrive(second[2])
        b_fwd(1, second[2], 3).start()
        b_own(0, second[3], 3).start()
        b_arrive(second[3])
        b_fwd(1, second[3], 3).start()
        multiply(0, m, x_ref, 0, half, n - half)
        l_gather_wait(1, 4)
        b_arrive(direct, 3)
        multiply(1, 4 * m, xst, top, top, unit)
        x_direct(3).start()
        l_gather_drain(1, 0)
        l_relay_drain(4)
        sent(32)

    def row1():
        enter_upper(0, 2)
        for piece in second + [direct]:
            b_own(1, piece, 0).start()
        await_below()
        for piece in first[:2]:
            b_own(1, piece, 2).start()
        b_load(1, 0, n).start()
        release_below(0, 2)
        l_gather_start(0, 2)

        def pass_on(piece):
            b_arrive(piece)
            b_fwd(0, piece, 2).start()

        pass_on(first[0])
        b_arrive(direct, slot=10)
        b_fwd(2, direct, 0).start()
        l_relay_start(1, 3)
        pass_on(first[1])
        b_own(1, first[2], 2).start()
        l_load(0).wait()
        l_gather_wait(0, 2)
        b_load(1, 0, n).wait()
        multiply(0, 2 * m, x_ref, 0, 0, 2 * unit)
        b_arrive(direct)
        l_gather_wait(1, 3)
        multiply(1, 3 * m, xst, top, top, unit)
        pass_on(first[2])
        b_own(1, first[3], 2).start()
        pass_on(first[3])
        x_direct(2).start()
        multiply(0, 2 * m, x_ref, 0, 2 * unit, half - 2 * unit)
        multiply(0, 2 * m, x_ref, 0, top, unit)
        l_gather_drain(2, 0)
        l_relay_drain(3)
        for piece in second_fine:
            b_arrive(piece)
            multiply(0, 2 * m, x_ref, 0, piece[0], piece[1])
        sent(27)

    def lower(p):
        o, u = 5 - p, 1 if p == 2 else 0
        s, so = p - 2, o - 2
        mine, others = (first, second) if p == 2 else (second, first)
        base = mine[0][0]
        enter_lower(u)
        b_load(p, base, half).start()

        @pl.when(holds(p + 1))
        def _():
            l_cross(1, u).start()
        b_own(p, direct, u, 10 if p == 2 else None).start()
        pl.semaphore_wait(go, 1)

        @pl.when(holds(p + 1))
        def _():
            l_cross(s, o).start()
        l_gather_start(s, p + 1)
        for piece in others:
            b_own(p, piece, o).start()
        l_relay_start(so, o + 1)
        l_load(s).wait()
        l_gather_wait(s, p + 1)
        l_gather_wait(so, o + 1)
        l_gather_drain(p + 1, 2)
        l_relay_drain(o + 1)
        b_load(p, base, half).wait()

        for piece in mine:
            b_arrive(piece, 3)
            start, w, _ = piece

            def away(t):
                multiply(so, (o + 1) * m, xst, base, base + t * back, back)
                x_back(base, t, o).start()
            each((start - base) // back, (start - base + w) // back, away)
            multiply(s, (p + 1) * m, x_ref, 0, start, w)

        sent(16)
        all_bytes(x_ref.at[:, pl.ds(0, half + unit)], x_recv)

    pl.when(row == 0)(row0)
    pl.when(row == 1)(row1)
    pl.when(row == 2)(functools.partial(lower, 2))
    pl.when(row == 3)(functools.partial(lower, 3))


def _store_body(v_ref, x_ref, sem):
    rows = v_ref.shape[0] // STORES
    copies = [pltpu.make_async_copy(v_ref.at[pl.ds(i * rows, rows), :], x_ref.at[pl.ds(i * rows, rows), :], sem.at[i])
              for i in range(STORES)]
    for copy in copies:
        copy.start()
    for copy in copies:
        copy.wait()


def solution(mesh):
    spec = P(("batch", "row"), "col")
    n_row, n_col = mesh.shape["row"], mesh.shape["col"]
    assert n_row == 4

    def local(l_block, b_block):
        m, n = b_block.shape
        k = n_row * m
        half = 7 * n // 16
        dma = pltpu.SemaphoreType.DMA
        x = pl.pallas_call(
            functools.partial(_body, n_row, n_col),
            out_shape=pltpu.VMEM((m, n), b_block.dtype),
            in_specs=[pl.BlockSpec(memory_space=pl.ANY)] * 2,
            out_specs=pl.BlockSpec(memory_space=pltpu.VMEM),
            scratch_shapes=[
                pltpu.VMEM((2, m, k), l_block.dtype),
                pltpu.VMEM((k, n), b_block.dtype),
                pltpu.VMEM((m, half), b_block.dtype),
                dma((2,)),
                dma(()),
                dma((2,)),
                dma(()),
                dma((11,)),
                dma(()),
                dma(()),
                dma(()),
                pltpu.SemaphoreType.REGULAR,
                pltpu.SemaphoreType.REGULAR,
                pltpu.SemaphoreType.REGULAR,
            ],
            compiler_params=pltpu.CompilerParams(
                collective_id=0, has_side_effects=True, vmem_limit_bytes=50 * 1024 * 1024),
            name="tri_ring",
        )(l_block, b_block)
        return pl.pallas_call(
            _store_body,
            out_shape=jax.ShapeDtypeStruct((m, n), b_block.dtype),
            in_specs=[pl.BlockSpec(memory_space=pltpu.VMEM)],
            out_specs=pl.BlockSpec(memory_space=pl.ANY),
            scratch_shapes=[dma((STORES,))],
            compiler_params=pltpu.CompilerParams(vmem_limit_bytes=1024 * 1024),
            name="tri_store",
        )(pltpu.with_memory_space_constraint(x, pltpu.VMEM))

    return jax.shard_map(local, mesh=mesh, in_specs=(spec, spec), out_specs=spec, check_vma=False)
```

time: 364 us -> 189 us (0.52)
  waiting for transfers between devices: 322 us -> 0 us
  Pallas kernels: 0 us -> 188 us
  matrix products: 26 us -> 0 us
  between operations: 13.4 us -> 0.19 us
    all_gather x2 -> x0, waiting for transfers between devices: 321 us -> none  [the longest x1 294 us: local_product(): b_strip = lax.all_gather(b_block, 'row', axis=0, tiled=True)]
    pallas_call x0 -> x2, Pallas kernels: none -> 188 us  [the longest x1 184 us: local(): pl.pallas_call(functools.partial(_body, n_row, n_col), out_shape=pltpu.VM...]
    dot_general x1 -> x0, matrix products: 26 us -> none  [local_product(): result = jnp.dot(l_strip, b_strip, preferred_element_type=jnp.float32)]
  transfers between devices with their start and end apart: 2 -> 0, of which waited for: 2 -> 0; matrix products, arithmetic and copies ran while one was open for 0% -> 0% of each run, Pallas kernels for 0% -> 0%
where the time goes in v5:
time: 189 us; the launch traced here: 188 us
  Pallas kernels  188 us (99%)
    pallas_call x1, Pallas kernels, local(): pl.pallas_call(functools.partial(_body, n_row, n_col), out_shape=pltpu.VM...  184 us

profile of v5, /device:TPU:112, one launch (start us, length us, event | category | flops | bytes accessed | tf_op | source)
XLA Modules:
  0.0 187.7 jit_solution(16069193060104237704)
XLA Ops:
  0.0 184.1 %tri_ring.1.v_ref = bf16[512,8192]{1,0:T(8,128)(2,1)S(1)} custom-call(bf16[512,256]{1,0:T(8,128)(2,1)} %l_ref.1, bf16[512,8192]{1,0:T(8,128)(2,1)} %b_ref.1), custom_call_target="tpu_custom_call" | custom-call | tf_op jit(solution)/shard_map/tri_ring/pallas_call | solution.py:327
  184.2 3.4 %tri_store.1 = bf16[512,8192]{1,0:T(8,128)(2,1)} custom-call(bf16[512,8192]{1,0:T(8,128)(2,1)S(1)} %tri_ring.1.v_ref), custom_call_target="tpu_custom_call" | custom-call | tf_op jit(solution)/shard_map/tri_store/pallas_call | solution.py:352
